TPU v7x, 32 devices: a whole 2x2x4 slice. The times are simulated.
32 devices in a mesh: expert: 8 (over y, x, core), row: 4 (over z).
Axes of the slice: x: 2, y: 2, z: 4, core: 2. Of those that a mesh axis runs over, the one named last changes fastest.
Arguments:
- weights: bfloat16 [8, 7168, 2048], P('expert', 'row'), may hold values from -6 to 6
- left_bits: int32 [8, 7168], P('expert', 'row'), may hold values from 0 to 1
- right_bits: int32 [8, 2048], P('expert'), may hold values from 0 to 1
- groups: int32 [8, 2048], P('expert'), may hold values from 0 to 15, never falling along the last dimension, each value on 1 to 256 neighbouring positions
Outputs:
- scaled: bfloat16 [8, 7168, 2048], P('expert', 'row')
- block_error: float32 [8, 7168, 256], P('expert', 'row')
- scales: float32 [8, 16], P('expert')
- expert_error: float32 [8], P('expert')
- total_error: float32 [], replicated
Inputs may be any that keep to these rules, and one draw needn't show every extreme that they name: Along each expert's 2048 columns the group number never falls; each of the 16 groups holds 1 to 256 columns.
All inputs are finite; a program needn't handle non-finite values.
Results may differ from a plain program's by a relative error of at most 0.0091.
Values may be sent and summed in bfloat16 or wider, within the bound.
No kernel may reach another device: no remote copies, remote signals or barrier semaphores. Data moves between devices by JAX's collectives and lax.ppermute only.
A program may use at most 192 MiB of HBM per device.

v0:
```python
import math
import jax
import jax.numpy as jnp
from jax import lax
from jax.sharding import PartitionSpec as P

D = 7168
FF = 2048
HB = 128
OUTER = 16
GROUPS = 16
BLOCKS = 56


def sylvester(order):
    row_index = jnp.arange(order, dtype=jnp.int32)[:, None]
    col_index = jnp.arange(order, dtype=jnp.int32)[None, :]
    common = jnp.bitwise_and(row_index, col_index)
    parity = jnp.zeros((order, order), jnp.int32)
    for bit_pos in range(order.bit_length() - 1):
        parity = parity + jnp.bitwise_and(jnp.right_shift(common, bit_pos), 1)
    return (1 - 2 * jnp.bitwise_and(parity, 1)).astype(jnp.float32)


def cosine_block(order):
    first = jnp.arange(order, dtype=jnp.float32)[:, None]
    second = jnp.arange(order, dtype=jnp.float32)[None, :]
    table = math.sqrt(2.0 / order) * jnp.cos(math.pi * (2.0 * second + 1.0) * first / (2.0 * order))
    return jnp.where(first == 0.0, table * math.sqrt(0.5), table)


def coset_error(values):
    nearest = jnp.floor(values + 0.5)
    offset = values - nearest
    squares = jnp.sum(offset * offset, axis=-1)
    largest = jnp.max(jnp.abs(offset), axis=-1)
    parity = jnp.mod(jnp.sum(nearest, axis=-1), 2.0)
    return jnp.where(parity > 0.5, squares + 1.0 - 2.0 * largest, squares)


def lattice_error(values):
    octets = values.reshape(values.shape[:-1] + (values.shape[-1] // 8, 8))
    return jnp.minimum(coset_error(octets), coset_error(octets - 0.5))


def row_transform(mixed_rows, row_hadamard):
    turned = jnp.einsum("eibf,bk->eikf", mixed_rows, row_hadamard, precision=lax.Precision.HIGHEST)
    return turned / math.sqrt(HB)


def weight_of_rows(first_row, count):
    positions = (first_row + jnp.arange(count, dtype=jnp.int32)).astype(jnp.float32)
    return (1.0 + 4.0 * (positions + 0.5) / D) / 3.0


def group_scale(rotated, group_cols):
    column_peak = jnp.max(jnp.abs(rotated), axis=1)
    group_ids = jnp.arange(GROUPS, dtype=jnp.int32)
    in_group = group_cols[:, None, :] == group_ids[None, :, None]
    partial_peak = jnp.max(jnp.where(in_group, column_peak[:, None, :], 0.0), axis=2)
    group_peak = jnp.maximum(lax.pmax(partial_peak, "row"), 1.0)
    column_scale = jnp.sum(jnp.where(in_group, (2.0 / group_peak)[:, :, None], 0.0), axis=1)
    return (group_peak, column_scale)


def body(weights, left_bits, right_bits, groups):
    experts, local_rows, width = weights.shape
    blocks_here = local_rows // HB
    column_hadamard = sylvester(width // OUTER).astype(jnp.bfloat16)
    outer_hadamard = sylvester(OUTER)
    row_hadamard = sylvester(HB)
    block_matrix = cosine_block(BLOCKS).astype(jnp.bfloat16)
    left_sign = (2 * left_bits - 1).astype(jnp.float32)
    right_sign = (2 * right_bits - 1).astype(jnp.float32)
    signed = (weights.astype(jnp.float32) * left_sign[:, :, None] * right_sign[:, None, :]).astype(
        jnp.bfloat16
    )
    shaped = signed.reshape(experts, local_rows, OUTER, width // OUTER)
    inner = jnp.einsum("erpq,qs->erps", shaped, column_hadamard, preferred_element_type=jnp.float32)
    outer = jnp.einsum("erps,pt->erts", inner, outer_hadamard, precision=lax.Precision.HIGHEST)
    columns = (outer.reshape(experts, local_rows, width) / math.sqrt(FF)).astype(jnp.bfloat16)
    blocked = columns.reshape(experts, blocks_here, HB, width)
    own_start = lax.axis_index("row") * blocks_here
    own_matrix = lax.dynamic_slice_in_dim(block_matrix, own_start, blocks_here, 0)
    mixed_rows = jnp.einsum(
        "ij,ejbf->eibf",
        own_matrix,
        lax.all_gather(blocked, "row", axis=1, tiled=True),
        preferred_element_type=jnp.float32,
    )
    rotated = row_transform(mixed_rows, row_hadamard)
    rotated = rotated.reshape(experts, local_rows, width)
    group_peak, column_scale = group_scale(rotated, groups)
    values = rotated * column_scale[:, None, :]
    block_errors = lattice_error(values)
    row_weight = weight_of_rows(lax.axis_index("row") * local_rows, local_rows)
    partial_error = jnp.sum(block_errors * row_weight[None, :, None], axis=(1, 2)) / (D * FF // 8)
    scaled = values.astype(jnp.bfloat16)
    expert_count = experts * lax.axis_size("expert")
    expert_error = lax.psum(partial_error, "row")
    total_error = lax.psum(jnp.sum(expert_error), "expert") / expert_count
    return (scaled, block_errors, group_peak / 2.0, expert_error, total_error)


def solution(mesh):
    placed = (P("expert", "row", None), P("expert", "row"), P("expert", None), P("expert", None))
    return jax.shard_map(
        body,
        mesh=mesh,
        in_specs=placed,
        out_specs=(
            P("expert", "row", None),
            P("expert", "row", None),
            P("expert", None),
            P("expert"),
            P(),
        ),
        check_vma=False,
    )
```

profile of v0, /device:TPU:0, one launch (start us, length us, event | category | flops | bytes accessed | tf_op | source)
XLA Modules:
  0.0 734.2 jit_solution(6547402217888224501)
XLA Ops:
  7.2 0.0 all-gather.2.cloned.1.call-start
  7.2 0.7 add_convert_fusion
  7.9 0.7 convert_reduce_fusion
  8.6 5.1 fusion.8
  13.7 5.8 copy.28
  19.5 4.3 fusion.25
  23.9 15.7 %fusion.14 = bf16[1,1792,16,128]{3,2,1,0:T(8,128)(2,1)} fusion(f32[1792,16,128]{2,1,0:T(8,128)S(1)} %fusion.25), kind=kOutput, calls=%fused_computation.22 | convolution fusion | flops 711987200 | bytes 22020096 | tf_op jit(solution)/shard_map/erps,pt->erts/dot_general | solution.py:80
  39.6 11.8 %convert_element_type.76 = bf16[1,14,128,2048]{3,2,1,0:T(8,128)(2,1)} reshape(bf16[1,1792,16,128]{3,2,1,0:T(8,128)(2,1)} %fusion.14) | data formatting | bytes 14680064 | tf_op jit(solution)/shard_map/convert_element_type | solution.py:81
  51.4 0.0 all-gather.2.cloned.1.call-update
  51.4 0.1 dynamic-slice
  51.5 495.9 %all-gather.2.cloned.1.call-done = bf16[1,56,128,2048]{3,2,0,1:T(8,128)(2,1)} async-done(((bf16[1,14,128,2048]{3,2,0,1:T(8,128)(2,1)}), bf16[1,56,128,2048]{3,2,0,1:T(8,128)(2,1)}) %all-gather.2.cloned.1.call-update) | async-done | bytes 29360144 | tf_op jit(solution)/shard_map/all_gather | solution.py:88
  547.4 31.9 %fusion.9 = f32[14,128,2048]{2,0,1:T(8,128)} fusion(bf16[1,56,128,2048]{3,2,0,1:T(8,128)(2,1)} %all-gather.2.cloned.1.call-done, s32[]{:T(128)S(6)} %select_n.94, f32[56]{0:T(128)S(1)} %add_multiply_fusion.2, pred[14]{0:T(512)(128)(4,1)S(1)} %dynamic-slice), kind=kOutput, calls=%fused_computation.21 | convolution fusion | flops 411048064 | bytes 44040432 | tf_op jit(solution)/shard_map/ij,ejbf->eibf/dot_general | solution.py:85
  579.3 0.0 copy-start
  579.3 29.6 %abs_reduce_fusion.2 = (f32[2048]{0:T(1024)S(1)}, f32[128,14,2048]{2,0,1:T(8,128)}) fusion(f32[14,128,2048]{2,0,1:T(8,128)} %fusion.9), kind=kOutput, calls=%fused_computation.15 | convolution fusion | flops 5648562176 | bytes 29368320 | tf_op jit(solution)/shard_map/eibf,bk->eikf/dot_general | solution.py:47
  608.9 0.0 copy-done
  608.9 0.1 select_reduce_fusion.1
  609.0 8.9 %pmax.7 = f32[1,16]{1,0:T(1,128)S(1)} all-reduce(f32[1,16]{1,0:T(1,128)S(1)} %bitcast.114), channel_id=1, replica_groups=mesh['expert'=8,'row'=4] {'row'}, use_global_device_ids=true, to_apply=%region_2.3 | all-reduce | flops 16 | bytes 128 | tf_op jit(solution)/shard_map/pmax | solution.py:61
  617.9 0.5 maximum_multiply_fusion
  618.4 0.1 select_reduce_fusion
  618.5 0.1 mul.276
  618.6 10.4 %fusion.3 = bf16[1,1792,2048]{2,1,0:T(8,128)(2,1)} fusion(f32[128,14,2048]{2,0,1:T(8,128)} %get-tuple-element.26, f32[2048]{0:T(1024)S(1)} %select_reduce_fusion), kind=kLoop, calls=%fused_computation.4 | loop fusion | flops 7340032 | bytes 22028288 | tf_op jit(solution)/shard_map/convert_element_type | solution.py:98
  629.0 17.6 %copy.24 = f32[1,14,128,2048]{2,1,3,0:T(8,128)} copy(f32[1,14,128,2048]{3,2,1,0:T(8,128)} %bitcast.108) | data formatting | bytes 29360128 | tf_op jit(solution)/shard_map/div | solution.py:48
  646.6 16.9 %reshape.599 = f32[1,1792,256,8]{1,3,2,0:T(8,128)} reshape(f32[1,14,128,2048]{2,1,3,0:T(8,128)} %copy.24) | data formatting | bytes 29360128 | tf_op jit(solution)/shard_map/reshape | solution.py:92
  663.5 32.5 %fusion.7 = (f32[1792,256]{0,1:T(8,128)S(1)}, f32[1792,256]{0,1:T(8,128)S(1)}, f32[1792,256]{0,1:T(8,128)S(1)}, f32[1792,256]{0,1:T(8,128)S(1)}, f32[1792,256]{0,1:T(8,128)S(1)}, /*index=5*/f32[1792,256]{0,1:T(8,128)S(1)}) fusion(f32[1,1792,256,8]{1,3,2,0:T(8,128)} %reshape.599, f32[256,8]{1,0:T(8,128)S(1)} %mul.276), kind=kLoop, calls=%fused_computation.14 | loop fusion | flops 59637760 | bytes 25698304 | tf_op jit(solution)/shard_map/reduce_sum | solution.py:37
  696.0 3.2 multiply_reduce_fusion.2
  699.3 1.7 copy.25
  701.6 11.3 %psum.14 = f32[1]{0:T(128)} all-reduce(f32[1]{0:T(128)} %bitcast.25), channel_id=1, replica_groups=mesh['expert'=8,'row'=4] {'row'}, use_global_device_ids=true, to_apply=%region_11.12 | all-reduce | flops 1 | bytes 8 | tf_op jit(solution)/shard_map/psum | solution.py:100
  712.9 12.4 %psum.15 = f32[]{:T(128)} all-reduce(f32[]{:T(128)} %bitcast.26), channel_id=1, replica_groups=mesh['expert'=8,'row'=4] {'expert'}, use_global_device_ids=true, to_apply=%region_12.13 | all-reduce | flops 1 | bytes 8 | tf_op jit(solution)/shard_map/psum | solution.py:101
  (3 shorter events, 0.0 us)
Async XLA Ops:
  7.2 540.2 %all-gather.2.cloned.1.call-start = ((), (), s32[]{:S(2)}) async-start(), calls=%async_computation | async-start | bytes 36700160 | tf_op jit(solution)/shard_map/all_gather | solution.py:88
  579.3 29.6 %copy-start = (s32[1,2048]{1,0:T(1,128)S(1)}, s32[1,2048]{1,0:T(1,128)}, u32[]{:S(2)}) copy-start(s32[1,2048]{1,0:T(1,128)} %param.7) | copy-start | bytes 24580
Sparse Core Ops, SparseCore 0:
  51.5 495.8 all-gather.1
where the time goes:
time: 743 us; the launch traced here: 734 us
  waiting for transfers between devices  496 us (67%)
  matrix products  81.6 us (11%)
  local copies, waits for them, and re-layouts  53.9 us (7%)
  other arithmetic  53.5 us (7%)
  blocking collectives  32.6 us (4%)
  between operations  16.7 us (2%)
    all_gather x1, waiting for transfers between devices, body(): lax.all_gather(blocked, 'row', axis=1, tiled=True)  496 us
    reduce_sum x1, other arithmetic, coset_error(): parity = jnp.mod(jnp.sum(nearest, axis=-1), 2.0)  32.5 us
    dot_general x1, matrix products, body(): jnp.einsum('ij,ejbf->eibf', own_matrix, lax.all_gather(blocked, 'row', ax...  31.9 us
    dot_general x1, matrix products, row_transform(): jnp.einsum('eibf,bk->eikf', mixed_rows, row_hadamard, precision=lax.Preci...  29.6 us
    div x1, local copies, waits for them, and re-layouts, row_transform(): return turned / math.sqrt(HB)  17.6 us
    reshape x1, local copies, waits for them, and re-layouts, body(): rotated = rotated.reshape(experts, local_rows, width)  16.9 us
    dot_general x1, matrix products, body(): jnp.einsum('erps,pt->erts', inner, outer_hadamard, precision=lax.Precisio...  15.7 us
  transfers between devices with their start and end apart: 1, of which 1 were waited for; matrix products, arithmetic and copies ran while one was open for 0% of the time, Pallas kernels for 0%

commit v1 on v0

--- a/solution.py
+++ b/solution.py
@@ -82,12 +82,27 @@
     blocked = columns.reshape(experts, blocks_here, HB, width)
     own_start = lax.axis_index("row") * blocks_here
     own_matrix = lax.dynamic_slice_in_dim(block_matrix, own_start, blocks_here, 0)
-    mixed_rows = jnp.einsum(
+    size, index = (lax.axis_size("row"), lax.axis_index("row"))
+    downward = [(i, (i - 1) % size) for i in range(size)]
+    width_2 = blocked.shape[1]
+    held = blocked
+    total = jnp.einsum(
         "ij,ejbf->eibf",
-        own_matrix,
-        lax.all_gather(blocked, "row", axis=1, tiled=True),
+        lax.dynamic_slice_in_dim(own_matrix, index * width_2, held.shape[1], axis=1),
+        held,
         preferred_element_type=jnp.float32,
     )
+    for step in range(1, size):
+        held = lax.ppermute(held, "row", downward)
+        total = total + jnp.einsum(
+            "ij,ejbf->eibf",
+            lax.dynamic_slice_in_dim(
+                own_matrix, (index + step) % size * width_2, held.shape[1], axis=1
+            ),
+            held,
+            preferred_element_type=jnp.float32,
+        )
+    mixed_rows = total
     rotated = row_transform(mixed_rows, row_hadamard)
     rotated = rotated.reshape(experts, local_rows, width)
     group_peak, column_scale = group_scale(rotated, groups)

time: 743 us -> 723 us (0.973)
  waiting for transfers between devices: 496 us -> 420 us
  matrix products: 81.6 us -> 119 us
  local copies, waits for them, and re-layouts: 53.9 us -> 69 us
  starting transfers between devices: 0.04 us -> 13.6 us
  between operations: 16.7 us -> 3.39 us
    all_gather x1 -> x0, waiting for transfers between devices: 496 us -> none  [body(): lax.all_gather(blocked, 'row', axis=1, tiled=True)]
    ppermute x0 -> x3, waiting for transfers between devices: none -> 420 us  [body(): held = lax.ppermute(held, 'row', downward)]
    dot_general x1 -> x4, matrix products: 31.9 us -> 69.1 us  [the longest x3 55.6 us: body(): jnp.einsum('ij,ejbf->eibf', lax.dynamic_slice_in_dim(own_matrix, (index +...]
    ppermute x0 -> x3, starting transfers between devices: none -> 13.6 us  [body(): held = lax.ppermute(held, 'row', downward)]
    convert_element_type x1 -> x2, local copies, waits for them, and re-layouts: 11.8 us -> 23.9 us  [body(): (outer.reshape(experts, local_rows, width) / math.sqrt(FF)).astype(jnp.bf...]
  transfers between devices with their start and end apart: 1 -> 3, of which waited for: 1 -> 3; matrix products, arithmetic and copies ran while one was open for 0% -> 7% of each run, Pallas kernels for 0% -> 0%
where the time goes in v1:
time: 723 us; the launch traced here: 713 us
  waiting for transfers between devices  420 us (58%)
  matrix products  119 us (16%)
  local copies, waits for them, and re-layouts  69 us (10%)
  other arithmetic  53.6 us (7%)
  blocking collectives  34.8 us (5%)
  starting transfers between devices  13.6 us (2%)
    ppermute x3, waiting for transfers between devices, body(): held = lax.ppermute(held, 'row', downward)  420 us
    dot_general x3, matrix products, body(): jnp.einsum('ij,ejbf->eibf', lax.dynamic_slice_in_dim(own_matrix, (index +...  55.6 us
    reduce_sum x1, other arithmetic, coset_error(): parity = jnp.mod(jnp.sum(nearest, axis=-1), 2.0)  32.5 us
    dot_general x1, matrix products, row_transform(): jnp.einsum('eibf,bk->eikf', mixed_rows, row_hadamard, precision=lax.Preci...  29.8 us
    convert_element_type x2, local copies, waits for them, and re-layouts, body(): (outer.reshape(experts, local_rows, width) / math.sqrt(FF)).astype(jnp.bf...  23.9 us
    div x1, local copies, waits for them, and re-layouts, row_transform(): return turned / math.sqrt(HB)  17.6 us
    reshape x1, local copies, waits for them, and re-layouts, body(): rotated = rotated.reshape(experts, local_rows, width)  16.9 us
    dot_general x1, matrix products, body(): jnp.einsum('erps,pt->erts', inner, outer_hadamard, precision=lax.Precisio...  15.7 us
  transfers between devices with their start and end apart: 3, of which 3 were waited for; matrix products, arithmetic and copies ran while one was open for 7% of the time, Pallas kernels for 0%

profile of v1, /device:TPU:0, one launch (start us, length us, event | category | flops | bytes accessed | tf_op | source)
XLA Modules:
  0.0 713.5 jit_solution(14558997916857791400)
XLA Ops:
  0.6 0.7 add_convert_fusion
  1.3 0.7 convert_reduce_fusion
  2.1 5.1 fusion.16
  7.1 5.8 copy.34
  12.9 4.4 fusion.32
  17.3 15.7 %fusion.21 = bf16[1,1792,16,128]{3,2,1,0:T(8,128)(2,1)} fusion(f32[1792,16,128]{2,1,0:T(8,128)S(1)} %fusion.32), kind=kOutput, calls=%fused_computation.30 | convolution fusion | flops 711987200 | bytes 22020096 | tf_op jit(solution)/shard_map/erps,pt->erts/dot_general | solution.py:80
  33.0 11.8 %convert_element_type.90 = bf16[1,14,128,2048]{3,2,1,0:T(8,128)(2,1)} reshape(bf16[1,1792,16,128]{3,2,1,0:T(8,128)(2,1)} %fusion.21) | data formatting | bytes 14680064 | tf_op jit(solution)/shard_map/convert_element_type | solution.py:81
  44.8 5.1 collective-permute-start
  49.9 157.6 %collective-permute-done = bf16[1,14,128,2048]{3,2,1,0:T(8,128)(2,1)S(1)} collective-permute-done((bf16[1,14,128,2048]{3,2,1,0:T(8,128)(2,1)}, bf16[1,14,128,2048]{3,2,1,0:T(8,128)(2,1)S(1)}, u32[]{:S(2)}, u32[]{:S(2)}) %collective-permute-start) | collective-permute-done | bytes 7340064 | tf_op jit(solution)/shard_map/ppermute | solution.py:96
  207.5 3.0 copy-done
  210.4 4.2 collective-permute-start.1
  214.6 156.4 %collective-permute-done.1 = bf16[1,14,128,2048]{3,2,1,0:T(8,128)(2,1)} collective-permute-done((bf16[1,14,128,2048]{3,2,1,0:T(8,128)(2,1)S(1)}, bf16[1,14,128,2048]{3,2,1,0:T(8,128)(2,1)}, u32[]{:S(2)}, u32[]{:S(2)}) %collective-permute-start.1) | collective-permute-done | bytes 7340064 | tf_op jit(solution)/shard_map/ppermute | solution.py:96
  371.0 4.4 collective-permute-start.2
  375.4 12.1 %convert_element_type.88 = bf16[14,128,2048]{2,1,0:T(8,128)(2,1)} reshape(bf16[1,1792,16,128]{3,2,1,0:T(8,128)(2,1)} %fusion.21) | data formatting | bytes 14680064 | tf_op jit(solution)/shard_map/convert_element_type | solution.py:81
  387.6 0.1 select_convert_fusion
  387.7 13.5 %fusion.14 = f32[128,2048,14]{1,2,0:T(8,128)} fusion(bf16[14,128,2048]{2,1,0:T(8,128)(2,1)} %convert_element_type.88, bf16[56,56]{1,0:T(8,128)(2,1)S(1)} %select_convert_fusion, s32[]{:T(128)S(6)} %select_n.134), kind=kOutput, calls=%fused_computation.26 | convolution fusion | flops 102760448 | bytes 22024196 | tf_op jit(solution)/shard_map/ij,ejbf->eibf/dot_general | solution.py:89
  401.2 10.3 %fusion.9 = f32[128,2048,14]{1,2,0:T(8,128)} fusion(bf16[1,14,128,2048]{3,2,1,0:T(8,128)(2,1)S(1)} %bitcast.127, bf16[56,56]{1,0:T(8,128)(2,1)S(1)} %select_convert_fusion, s32[]{:T(128)S(6)} %select_n.134, s32[]{:T(128)S(6)} %select_n.137), kind=kOutput, calls=%fused_computation.21 | convolution fusion | flops 102760448 | bytes 22024200 | tf_op jit(solution)/shard_map/ij,ejbf->eibf/dot_general | solution.py:97
  411.5 13.5 %fusion.7 = f32[128,2048,14]{1,2,0:T(8,128)} fusion(bf16[1,14,128,2048]{3,2,1,0:T(8,128)(2,1)} %collective-permute-done.1, bf16[56,56]{1,0:T(8,128)(2,1)S(1)} %select_convert_fusion, s32[]{:T(128)S(6)} %select_n.134, s32[]{:T(128)S(6)} %select_n.140), kind=kOutput, calls=%fused_computation.19 | convolution fusion | flops 102760448 | bytes 22024200 | tf_op jit(solution)/shard_map/ij,ejbf->eibf/dot_general | solution.py:97
  425.0 106.2 %collective-permute-done.2 = bf16[1,14,128,2048]{3,2,1,0:T(8,128)(2,1)} collective-permute-done((bf16[1,14,128,2048]{3,2,1,0:T(8,128)(2,1)}, bf16[1,14,128,2048]{3,2,1,0:T(8,128)(2,1)}, u32[]{:S(2)}, u32[]{:S(2)}) %collective-permute-start.2) | collective-permute-done | bytes 7340064 | tf_op jit(solution)/shard_map/ppermute | solution.py:96
  531.2 31.9 %add_bitcast_fusion = f32[14,128,2048]{2,0,1:T(8,128)} fusion(f32[128,2048,14]{1,2,0:T(8,128)} %fusion.7, f32[128,2048,14]{1,2,0:T(8,128)} %fusion.14, f32[128,2048,14]{1,2,0:T(8,128)} %fusion.9, bf16[1,14,128,2048]{3,2,1,0:T(8,128)(2,1)} %collective-permute-done.2, bf16[56,56]{1,0:T(8,128)(2,1)S(1)} %select_convert_fusion, s32[]{:T(128)S(6)} %select_n.134, ...), kind=kOutput, calls=%fused_computation | convolution fusion | flops 113770496 | bytes 66064392 | tf_op jit(solution)/shard_map/ij,ejbf->eibf/dot_general | solution.py:97
  563.1 29.8 %abs_reduce_fusion.2 = (f32[2048]{0:T(1024)S(1)}, f32[128,14,2048]{2,0,1:T(8,128)}) fusion(f32[14,128,2048]{2,0,1:T(8,128)} %add_bitcast_fusion), kind=kOutput, calls=%fused_computation.13 | convolution fusion | flops 5648562176 | bytes 29368320 | tf_op jit(solution)/shard_map/eibf,bk->eikf/dot_general | solution.py:47
  592.9 0.1 select_reduce_fusion.1
  593.0 12.8 %pmax.7 = f32[1,16]{1,0:T(1,128)S(1)} all-reduce(f32[1,16]{1,0:T(1,128)S(1)} %bitcast.131), channel_id=1, replica_groups=mesh['expert'=8,'row'=4] {'row'}, use_global_device_ids=true, to_apply=%region_2.3 | all-reduce | flops 16 | bytes 128 | tf_op jit(solution)/shard_map/pmax | solution.py:61
  605.8 0.5 maximum_multiply_fusion
  606.6 10.4 %fusion = bf16[1,1792,2048]{2,1,0:T(8,128)(2,1)} fusion(f32[128,14,2048]{2,0,1:T(8,128)} %get-tuple-element.26, f32[2048]{0:T(1024)S(1)} %select_reduce_fusion), kind=kLoop, calls=%fused_computation.2 | loop fusion | flops 7340032 | bytes 22028288 | tf_op jit(solution)/shard_map/convert_element_type | solution.py:113
  617.0 17.6 %copy.30 = f32[1,14,128,2048]{2,1,3,0:T(8,128)} copy(f32[1,14,128,2048]{3,2,1,0:T(8,128)} %bitcast.124) | data formatting | bytes 29360128 | tf_op jit(solution)/shard_map/div | solution.py:48
  634.6 16.9 %reshape.621 = f32[1,1792,256,8]{1,3,2,0:T(8,128)} reshape(f32[1,14,128,2048]{2,1,3,0:T(8,128)} %copy.30) | data formatting | bytes 29360128 | tf_op jit(solution)/shard_map/reshape | solution.py:107
  651.5 32.5 %fusion.4 = (f32[1792,256]{0,1:T(8,128)S(1)}, f32[1792,256]{0,1:T(8,128)S(1)}, f32[1792,256]{0,1:T(8,128)S(1)}, f32[1792,256]{0,1:T(8,128)S(1)}, f32[1792,256]{0,1:T(8,128)S(1)}, /*index=5*/f32[1792,256]{0,1:T(8,128)S(1)}) fusion(f32[1,1792,256,8]{1,3,2,0:T(8,128)} %reshape.621, f32[256,8]{1,0:T(8,128)S(1)} %mul.331), kind=kLoop, calls=%fused_computation.12 | loop fusion | flops 59637760 | bytes 25698304 | tf_op jit(solution)/shard_map/reduce_sum | solution.py:37
  684.0 3.2 multiply_reduce_fusion.2
  687.3 1.7 copy.31
  689.6 9.5 %psum.14 = f32[1]{0:T(128)} all-reduce(f32[1]{0:T(128)} %bitcast.30), channel_id=1, replica_groups=mesh['expert'=8,'row'=4] {'row'}, use_global_device_ids=true, to_apply=%region_11.12 | all-reduce | flops 1 | bytes 8 | tf_op jit(solution)/shard_map/psum | solution.py:115
  699.1 12.4 %psum.15 = f32[]{:T(128)} all-reduce(f32[]{:T(128)} %bitcast.31), channel_id=1, replica_groups=mesh['expert'=8,'row'=4] {'expert'}, use_global_device_ids=true, to_apply=%region_12.13 | all-reduce | flops 1 | bytes 8 | tf_op jit(solution)/shard_map/psum | solution.py:116
  (13 shorter events, 0.2 us)
Async XLA Ops:
  44.8 162.6 %collective-permute-start = (bf16[1,14,128,2048]{3,2,1,0:T(8,128)(2,1)}, bf16[1,14,128,2048]{3,2,1,0:T(8,128)(2,1)S(1)}, u32[]{:S(2)}, u32[]{:S(2)}) collective-permute-start(bf16[1,14,128,2048]{3,2,1,0:T(8,128)(2,1)} %convert_element_type.90), channel_id=1, source_target_pairs={{0,3},{1,0},{2,1},{3,2},{4,7},{5,4},{6,5},{7,6},{8,11},{9,8},{10,9... | collective-permute-start | bytes 22020104 | tf_op jit(solution)/shard_map/ppermute | solution.py:96
  207.4 3.0 copy-start
  210.4 160.6 %collective-permute-start.1 = (bf16[1,14,128,2048]{3,2,1,0:T(8,128)(2,1)S(1)}, bf16[1,14,128,2048]{3,2,1,0:T(8,128)(2,1)}, u32[]{:S(2)}, u32[]{:S(2)}) collective-permute-start(bf16[1,14,128,2048]{3,2,1,0:T(8,128)(2,1)S(1)} %collective-permute-done), channel_id=1, source_target_pairs={{0,3},{1,0},{2,1},{3,2},{4,7},{5,4},{6,5},{7,6},{8,11},{9,8},{10,9... | collective-permute-start | bytes 22020104 | tf_op jit(solution)/shard_map/ppermute | solution.py:96
  371.0 160.2 %collective-permute-start.2 = (bf16[1,14,128,2048]{3,2,1,0:T(8,128)(2,1)}, bf16[1,14,128,2048]{3,2,1,0:T(8,128)(2,1)}, u32[]{:S(2)}, u32[]{:S(2)}) collective-permute-start(bf16[1,14,128,2048]{3,2,1,0:T(8,128)(2,1)} %collective-permute-done.1), channel_id=1, source_target_pairs={{0,3},{1,0},{2,1},{3,2},{4,7},{5,4},{6,5},{7,6},{8,11},{9,8},{10,9... | collective-permute-start | bytes 22020104 | tf_op jit(solution)/shard_map/ppermute | solution.py:96
  375.4 25.8 %slice-start = ((s8[7340032]{0:T(1024)(128)(4,1)}), s8[3145728]{0:T(1024)(128)(4,1)S(1)}, s32[]{:S(2)}) async-start(s8[7340032]{0:T(1024)(128)(4,1)} %bitcast.126), calls=%async_computation | async-start | bytes 6291456
  387.7 13.5 %slice-start.1 = ((s8[7340032]{0:T(1024)(128)(4,1)}), s8[4194304]{0:T(1024)(128)(4,1)S(1)}, s32[]{:S(2)}) async-start(s8[7340032]{0:T(1024)(128)(4,1)} %bitcast.126), calls=%async_computation.1 | async-start | bytes 8388608
  563.1 29.8 %copy-start.1 = (s32[1,2048]{1,0:T(1,128)S(1)}, s32[1,2048]{1,0:T(1,128)}, u32[]{:S(2)}) copy-start(s32[1,2048]{1,0:T(1,128)} %param.7) | copy-start | bytes 24580
